TPU v7x, 32 devices: a whole 2x2x4 slice. The times are simulated.
32 devices in a mesh: kv: 16 (over z, y, x), head: 2 (over core).
Axes of the slice: x: 2, y: 2, z: 4, core: 2. Of those that a mesh axis runs over, the one named last changes fastest.
Arguments:
- queries: bfloat16 [8, 256, 128], P('head', 'kv'), may hold values from -384 to 384
- key_cache: bfloat16 [4096, 8, 128, 128], P('kv', 'head'), may hold values from -6 to 6
- value_cache: bfloat16 [4096, 8, 128, 128], P('kv', 'head'), may hold values from -6 to 6
- key_new: bfloat16 [32, 8, 128], P(None, 'head'), may hold values from -6 to 6
- value_new: bfloat16 [32, 8, 128], P(None, 'head'), may hold values from -6 to 6
- lengths: int32 [32], replicated, may hold values from 2 to 16385, as said below
- page_table: int32 [4096], replicated, may hold values from 0 to 4095, each once
Outputs:
- attended: bfloat16 [8, 256, 128], P('head', 'kv')
Inputs may be any that keep to these rules, and one draw needn't show every extreme that they name: The cache holds the first lengths[s] - 1 tokens of sequence s; some sequence has the largest length. `page_table`: every page appears once; page g lies on kv index g // 256.
All inputs are finite; a program needn't handle non-finite values.
Results may differ from a plain program's by a relative error of at most 0.0025.
Values may be sent and summed in bfloat16 or wider, within the bound.
A program may use at most 128 MiB of HBM per device.

v0:
```python
import functools
import math

import jax
import jax.numpy as jnp
from jax import lax
from jax.experimental import pallas as pl
from jax.experimental.pallas import tpu as pltpu
from jax.sharding import PartitionSpec as P

LOWEST_SCORE = -1e30
MESH = pl.DeviceIdType.MESH
VMEM = pltpu.VMEM

GROUP = 8
RING = 4

_dot = functools.partial(lax.dot_general, preferred_element_type=jnp.float32)
NT = (((1,), (1,)), ((), ()))
NN = (((1,), (0,)), ((), ()))


def greet(peers):
    barrier = pltpu.get_barrier_semaphore()
    for peer in peers:
        pl.semaphore_signal(barrier, inc=1, device_id={"kv": peer}, device_id_type=MESH)
    pl.semaphore_wait(barrier, len(peers))


def gather_kernel(
    n,
    pages_here,
    page_len,
    x_ref,
    table_ref,
    length_ref,
    all_ref,
    list_ref,
    send_sem,
    recv_sem,
    own_sem,
):
    me = lax.axis_index("kv")
    own = pltpu.make_async_copy(x_ref, all_ref.at[me], own_sem)
    own.start()
    greet([lax.rem(me + k, n) for k in range(1, n)])
    copies = []
    for k in range(1, n):
        copy = pltpu.make_async_remote_copy(
            src_ref=x_ref,
            dst_ref=all_ref.at[me],
            send_sem=send_sem.at[k],
            recv_sem=recv_sem.at[me],
            device_id={"kv": lax.rem(me + k, n)},
            device_id_type=MESH,
        )
        copy.start()
        copies.append(copy)
    list_pages(me, pages_here, page_len, table_ref, length_ref, list_ref)
    own.wait()
    for k in range(1, n):
        source = lax.rem(me + k, n)
        pltpu.make_async_remote_copy(
            src_ref=x_ref,
            dst_ref=all_ref.at[source],
            send_sem=send_sem.at[k],
            recv_sem=recv_sem.at[source],
            device_id={"kv": source},
            device_id_type=MESH,
        ).wait_recv()
    for copy in copies:
        copy.wait_send()


def list_pages(me, pages_here, page_len, table_ref, length_ref, list_ref):
    seqs, slots = table_ref.shape
    listed = list_ref.shape[1]
    page = table_ref[...] - me * pages_here
    line = lax.broadcasted_iota(jnp.int32, (seqs, slots), 0)
    length = jnp.zeros((seqs, slots), jnp.int32)
    for s in range(seqs):
        length = jnp.where(line == s, length_ref[s], length)
    tokens = length - 1 - lax.broadcasted_iota(jnp.int32, (seqs, slots), 1) * page_len
    wanted = (page >= 0) & (page < pages_here) & (tokens > 0)
    flag = jnp.where(wanted, 1.0, 0.0)
    upto = jnp.where(
        lax.broadcasted_iota(jnp.int32, (slots, slots), 0)
        <= lax.broadcasted_iota(jnp.int32, (slots, slots), 1),
        1.0,
        0.0,
    ).astype(jnp.bfloat16)
    inside = _dot(flag.astype(jnp.bfloat16), upto, NN)
    total = jnp.broadcast_to(jnp.sum(flag, axis=1, keepdims=True), (seqs, slots))
    before = jnp.where(
        lax.broadcasted_iota(jnp.int32, (seqs, seqs), 1)
        < lax.broadcasted_iota(jnp.int32, (seqs, seqs), 0),
        1.0,
        0.0,
    ).astype(jnp.bfloat16)
    offset = _dot(before, total.astype(jnp.bfloat16), NN)
    rank = jnp.where(wanted, inside + offset - 1.0, -1.0).astype(jnp.int32)
    wide = jnp.where(wanted, page, 0).astype(jnp.float32)
    held = jnp.where(wanted, jnp.minimum(tokens, page_len), 0).astype(jnp.float32)
    row = lax.broadcasted_iota(jnp.int32, (8, slots), 0)
    slot = lax.broadcasted_iota(jnp.int32, (8, slots), 1).astype(jnp.float32)
    place = lax.broadcasted_iota(jnp.int32, (listed, slots), 0)
    out = jnp.zeros((8, listed), jnp.float32)
    for s in range(seqs):
        values = jnp.where(
            row == 0,
            float(s),
            jnp.where(
                row == 1,
                slot,
                jnp.where(
                    row == 2,
                    jnp.broadcast_to(wide[s : s + 1], (8, slots)),
                    jnp.where(row == 3, jnp.broadcast_to(held[s : s + 1], (8, slots)), 0.0),
                ),
            ),
        ).astype(jnp.bfloat16)
        chosen = jnp.where(
            place == jnp.broadcast_to(rank[s : s + 1], (listed, slots)), 1.0, 0.0
        ).astype(jnp.bfloat16)
        out = out + _dot(values, chosen, NT)
    count = jnp.sum(jnp.sum(flag, axis=1, keepdims=True), axis=0, keepdims=True)
    out = jnp.where(
        lax.broadcasted_iota(jnp.int32, (8, listed), 0) == 4,
        jnp.broadcast_to(count, (8, listed)),
        out,
    )
    list_ref[...] = out.astype(jnp.int32)


def attend_kernel(
    group_rows,
    blocks,
    list_ref,
    q_ref,
    keys,
    values,
    out_ref,
    q_wide,
    key_buf,
    value_buf,
    best,
    weight,
    total,
    key_sem,
    value_sem,
):
    heads, page_len, width = key_buf.shape[2:]
    seqs = q_wide.shape[0]
    per_block = seqs // blocks
    scale2 = math.log2(math.e) / math.sqrt(width)
    count = list_ref[4, 0]
    groups = (count + GROUP - 1) // GROUP

    def copies(g, i):
        at = g * GROUP + i
        page = list_ref[2, at]
        slot = lax.rem(g, RING)
        return (
            pltpu.make_async_copy(keys.at[page], key_buf.at[slot, i], key_sem.at[slot, i]),
            pltpu.make_async_copy(values.at[page], value_buf.at[slot, i], value_sem.at[slot, i]),
        )

    def start(g):
        for i in range(GROUP):
            for copy in copies(g, i):
                copy.start()

    for g in range(RING - 1):
        pl.when(g < groups)(functools.partial(start, g))

    best[...] = jnp.full(best.shape, LOWEST_SCORE, jnp.float32)
    weight[...] = jnp.zeros(weight.shape, jnp.float32)
    total[...] = jnp.zeros(total.shape, jnp.float32)
    if q_ref.ndim == 4 and q_ref.shape[2] % group_rows == 0:
        each = q_ref.shape[2] // group_rows
        for d in range(q_ref.shape[0]):
            for h in range(heads):
                block = q_ref[d, h].astype(jnp.float32)
                for j in range(each):
                    q_wide[d * each + j, h] = block[j * group_rows : (j + 1) * group_rows]
    else:
        for d in range(q_ref.shape[0]):
            for h in range(heads):
                rows = q_ref.shape[2]
                parts = group_rows // rows
                q_wide[d // parts, h, (d % parts) * rows : (d % parts + 1) * rows] = q_ref[
                    d, h
                ].astype(jnp.float32)

    lane = lax.broadcasted_iota(jnp.int32, (group_rows, page_len), 1)

    def step(g, carry):
        pl.when(g + RING - 1 < groups)(lambda: start(g + RING - 1))
        slot = lax.rem(g, RING)
        for i in range(GROUP):
            for copy in copies(g, i):
                copy.wait()
        seq = [list_ref[0, g * GROUP + i] for i in range(GROUP)]
        inside = [lane < list_ref[3, g * GROUP + i] for i in range(GROUP)]
        both = [(i, pair) for i in range(GROUP) for pair in range(0, heads, 2)]
        each = [(i, h) for i in range(GROUP) for h in range(heads)]
        scores = {}
        for i, pair in both:
            q2 = q_wide[seq[i], pair : pair + 2].reshape(2 * group_rows, width)
            k2 = key_buf[slot, i, pair : pair + 2].reshape(2 * page_len, width)
            found = _dot(q2.astype(jnp.bfloat16), k2, NT)
            for e in range(2):
                scores[i, pair + e] = found[
                    e * group_rows : (e + 1) * group_rows, e * page_len : (e + 1) * page_len
                ]
        tops, lines = {}, {}
        for i, h in each:
            sc = jnp.where(inside[i], scores[i, h], LOWEST_SCORE)
            scores[i, h] = sc
            tops[i, h] = jnp.broadcast_to(jnp.max(sc, axis=1, keepdims=True), sc.shape)
        for i, h in each:
            lines[i, h] = jnp.where(
                inside[i], jnp.exp2((scores[i, h] - tops[i, h]) * scale2), 0.0
            )
        outs = {}
        for i, pair in both:
            w2 = jnp.concatenate([lines[i, pair], lines[i, pair + 1]], axis=0)
            v2 = jnp.concatenate(
                [value_buf[slot, i, pair], value_buf[slot, i, pair + 1]], axis=1
            )
            found = _dot(w2.astype(jnp.bfloat16), v2, NN)
            for e in range(2):
                outs[i, pair + e] = found[
                    e * group_rows : (e + 1) * group_rows, e * width : (e + 1) * width
                ]
        for i, h in each:
            s = seq[i]
            old = best[s, h]
            new = jnp.maximum(old, tops[i, h])
            keep = jnp.exp2((old - new) * scale2)
            add = jnp.exp2((tops[i, h] - new) * scale2)
            best[s, h] = new
            weight[s, h] = weight[s, h] * keep + lines[i, h] * add
            total[s, h] = total[s, h] * keep + outs[i, h] * add
        return carry

    lax.fori_loop(0, groups, step, 0)

    stat_lane = lax.broadcasted_iota(jnp.int32, (group_rows, width), 1)
    columns = heads * per_block
    for b in range(blocks):
        stats = jnp.zeros((group_rows, width), jnp.float32)
        for j in range(per_block):
            s = b * per_block + j
            for h in range(heads):
                at = h * per_block + j
                out_ref[b, at] = total[s, h]
                mass = jnp.sum(weight[s, h], axis=1, keepdims=True)
                stats = jnp.where(stat_lane == at, best[s, h], stats)
                stats = jnp.where(
                    stat_lane == columns + at, jnp.broadcast_to(mass, stats.shape), stats
                )
        out_ref[b, columns] = stats


def fold(pieces, columns, scale2):
    stats = [piece[columns] for piece in pieces]
    top = functools.reduce(jnp.maximum, stats)
    mass = jnp.zeros_like(top)
    sums = [jnp.zeros_like(top) for _ in range(columns)]
    for piece, own in zip(pieces, stats):
        factor = jnp.exp2((own - top) * scale2)
        mass = mass + own * pltpu.roll(factor, columns, 1)
        for c in range(columns):
            sums[c] = sums[c] + piece[c] * jnp.broadcast_to(factor[:, c : c + 1], top.shape)
    return top, mass, sums


def exchange_kernel(
    n,
    plane,
    parts,
    part_ref,
    q_ref,
    key_ref,
    value_ref,
    out_ref,
    near,
    folded,
    far,
    near_send,
    near_recv,
    far_send,
    far_recv,
    own_sem,
):
    me = lax.axis_index("kv")
    lines = n // plane
    spot, line = lax.rem(me, plane), me // plane
    tiles, group_rows, width = folded.shape[1:]
    columns = tiles - 1
    heads = q_ref.shape[0]
    per_block = columns // heads
    scale2 = math.log2(math.e) / math.sqrt(width)
    spots = [lax.rem(spot + k, plane) for k in range(1, plane)]
    turns = list(range(lines // 2, lines)) + list(range(lines // 2 - 1, 0, -1)) + [0]
    floors = [lax.rem(line + k, lines) for k in turns]
    own = []
    for k, floor in enumerate(floors):
        copy = pltpu.make_async_copy(
            part_ref.at[(floor * plane + spot) // parts], near.at[floor, spot], own_sem.at[k]
        )
        copy.start()
        own.append(copy)
    greet([line * plane + p for p in spots] + [f * plane + spot for f in floors[:-1]])
    copies = []
    for k, floor in enumerate(floors):
        for p, other in enumerate(spots):
            copy = pltpu.make_async_remote_copy(
                src_ref=part_ref.at[(floor * plane + other) // parts],
                dst_ref=near.at[floor, spot],
                send_sem=near_send.at[k, p],
                recv_sem=near_recv.at[floor, spot],
                device_id={"kv": line * plane + other},
                device_id_type=MESH,
            )
            copy.start()
            copies.append(copy)
    for k, floor in enumerate(floors):
        own[k].wait()
        for p, other in enumerate(spots):
            pltpu.make_async_remote_copy(
                src_ref=part_ref.at[(floor * plane + other) // parts],
                dst_ref=near.at[floor, other],
                send_sem=near_send.at[k, p],
                recv_sem=near_recv.at[floor, other],
                device_id={"kv": line * plane + other},
                device_id_type=MESH,
            ).wait_recv()
        top, mass, sums = fold([near.at[floor, p] for p in range(plane)], columns, scale2)
        stat_lane = lax.broadcasted_iota(jnp.int32, top.shape, 1)
        stats = jnp.where(stat_lane < columns, top, mass)
        for c in range(columns):
            folded[k, c] = sums[c]
        folded[k, columns] = stats
        if k < lines - 1:
            copy = pltpu.make_async_remote_copy(
                src_ref=folded.at[k],
                dst_ref=far.at[line],
                send_sem=far_send.at[k],
                recv_sem=far_recv.at[line],
                device_id={"kv": floor * plane + spot},
                device_id_type=MESH,
            )
            copy.start()
            copies.append(copy)
    for k, floor in enumerate(floors[:-1]):
        pltpu.make_async_remote_copy(
            src_ref=folded.at[k],
            dst_ref=far.at[floor],
            send_sem=far_send.at[k],
            recv_sem=far_recv.at[floor],
            device_id={"kv": floor * plane + spot},
            device_id_type=MESH,
        ).wait_recv()
    top, mass, sums = fold(
        [folded.at[lines - 1]] + [far.at[floor] for floor in floors[:-1]], columns, scale2
    )
    for h in range(heads):
        wide = q_ref[h].astype(jnp.float32)
        results = []
        for j in range(per_block):
            c = h * per_block + j
            s = (me // parts) * per_block + j
            rows = slice(j * group_rows, (j + 1) * group_rows) if parts == 1 else slice(None)
            query = wide[rows]
            shape = query.shape
            fresh_key = jnp.broadcast_to(key_ref[s][h : h + 1].astype(jnp.float32), shape)
            fresh_value = jnp.broadcast_to(value_ref[s][h : h + 1].astype(jnp.float32), shape)
            new = jnp.broadcast_to(jnp.sum(query * fresh_key, axis=1, keepdims=True), shape)

            def mine(x):
                if parts == 1:
                    return x
                size = group_rows // parts
                picked = x[:size]
                for p in range(1, parts):
                    picked = jnp.where(
                        lax.rem(me, parts) == p, x[p * size : (p + 1) * size], picked
                    )
                return picked

            old = mine(jnp.broadcast_to(top[:, c : c + 1], top.shape))
            old_mass = mine(jnp.broadcast_to(mass[:, columns + c : columns + c + 1], top.shape))
            old_sum = mine(sums[c])
            highest = jnp.maximum(old, new)
            old_part = jnp.exp2((old - highest) * scale2)
            new_part = jnp.exp2((new - highest) * scale2)
            results.append(
                (old_sum * old_part + new_part * fresh_value) / (old_mass * old_part + new_part)
            )
        out_ref[h] = jnp.concatenate(results, axis=0).astype(out_ref.dtype)
    for copy in copies:
        copy.wait_send()


def on_device(n, queries, key_cache, value_cache, key_new, value_new, lengths, page_table):
    heads, local_rows, width = queries.shape
    seqs = lengths.shape[0]
    slots = page_table.shape[0] // seqs
    pages_here, _, page_len, _ = key_cache.shape
    group_rows = local_rows * n // seqs
    parts = max(1, group_rows // local_rows)
    blocks = n // parts
    tiles = heads * (seqs // blocks) + 1
    listed = -(-pages_here // 128) * 128 + 128
    vmem = pl.BlockSpec(memory_space=VMEM)
    smem = pl.BlockSpec(memory_space=pltpu.SMEM)
    hbm = pl.BlockSpec(memory_space=pl.ANY)

    every_query, pages = pl.pallas_call(
        functools.partial(gather_kernel, n, pages_here, page_len),
        out_shape=(
            jax.ShapeDtypeStruct((n,) + queries.shape, queries.dtype),
            jax.ShapeDtypeStruct((8, listed), jnp.int32),
        ),
        in_specs=[vmem, vmem, smem],
        out_specs=(vmem, vmem),
        scratch_shapes=[
            pltpu.SemaphoreType.DMA((n,)),
            pltpu.SemaphoreType.DMA((n,)),
            pltpu.SemaphoreType.DMA,
        ],
        compiler_params=pltpu.CompilerParams(
            collective_id=0, has_side_effects=True, vmem_limit_bytes=16 * 1024 * 1024
        ),
        name="gather_queries",
    )(queries, page_table.reshape(seqs, slots), lengths)

    part = pl.pallas_call(
        functools.partial(attend_kernel, group_rows, blocks),
        out_shape=jax.ShapeDtypeStruct((blocks, tiles, group_rows, width), jnp.float32),
        in_specs=[smem, vmem, hbm, hbm],
        out_specs=vmem,
        scratch_shapes=[
            VMEM((seqs, heads, group_rows, width), jnp.float32),
            VMEM((RING, GROUP, heads, page_len, width), key_cache.dtype),
            VMEM((RING, GROUP, heads, page_len, width), value_cache.dtype),
            VMEM((seqs, heads, group_rows, page_len), jnp.float32),
            VMEM((seqs, heads, group_rows, page_len), jnp.float32),
            VMEM((seqs, heads, group_rows, width), jnp.float32),
            pltpu.SemaphoreType.DMA((RING, GROUP)),
            pltpu.SemaphoreType.DMA((RING, GROUP)),
        ],
        compiler_params=pltpu.CompilerParams(vmem_limit_bytes=48 * 1024 * 1024),
        name="attend_pages",
    )(pages, every_query, key_cache, value_cache)

    plane = min(p for p in range(1, n + 1) if n % p == 0 and p * p >= n)
    lines = n // plane
    tile = (tiles, group_rows, width)
    return pl.pallas_call(
        functools.partial(exchange_kernel, n, plane, parts),
        out_shape=jax.ShapeDtypeStruct(queries.shape, jnp.bfloat16),
        in_specs=[vmem] + [vmem] * 3,
        out_specs=vmem,
        scratch_shapes=[
            VMEM((lines, plane) + tile, jnp.float32),
            VMEM((lines,) + tile, jnp.float32),
            VMEM((lines,) + tile, jnp.float32),
            pltpu.SemaphoreType.DMA((lines, plane)),
            pltpu.SemaphoreType.DMA((lines, plane)),
            pltpu.SemaphoreType.DMA((lines,)),
            pltpu.SemaphoreType.DMA((lines,)),
            pltpu.SemaphoreType.DMA((lines,)),
        ],
        compiler_params=pltpu.CompilerParams(
            collective_id=1, has_side_effects=True, vmem_limit_bytes=16 * 1024 * 1024
        ),
        name="exchange_and_finish",
    )(part, queries, key_new, value_new)


def solution(mesh):
    placed = (
        P("head", "kv", None),
        P("kv", "head", None, None),
        P("kv", "head", None, None),
        P(None, "head", None),
        P(None, "head", None),
        P(),
        P(),
    )
    return jax.shard_map(
        functools.partial(on_device, mesh.shape["kv"]),
        mesh=mesh,
        in_specs=placed,
        out_specs=P("head", "kv", None),
        check_vma=False,
    )
```

profile of v0, /device:TPU:0, one launch (start us, length us, event | category | flops | bytes accessed | tf_op | source)
XLA Modules:
  0.0 46.7 jit_solution(14230096052325213264)
XLA Ops:
  0.0 0.0 copy-start
  0.0 0.7 %copy-done = bf16[4,16,128]{2,1,0:T(8,128)(2,1)S(1)} copy-done((bf16[4,16,128]{2,1,0:T(8,128)(2,1)S(1)}, bf16[4,16,128]{2,1,0:T(8,128)(2,1)}, u32[]{:S(2)}) %copy-start) | copy-done | bytes 16408
  0.7 0.0 copy-start.4
  0.7 0.7 %copy-done.4 = s32[4096]{0:T(1024)S(1)} copy-done((s32[4096]{0:T(1024)S(1)}, s32[4096]{0:T(1024)}, u32[]{:S(2)}) %copy-start.4) | copy-done | bytes 16408
  1.4 0.0 copy-start.5
  1.4 0.7 %copy-done.5 = s32[32]{0:T(128)S(1)} copy-done((s32[32]{0:T(128)S(1)}, s32[32]{0:T(128)}, u32[]{:S(2)}) %copy-start.5) | copy-done | bytes 152
  2.1 12.0 %gather_queries.1 = (bf16[16,4,16,128]{3,2,1,0:T(8,128)(2,1)S(1)}, s32[8,384]{1,0:T(8,128)S(1)}) custom-call(bf16[4,16,128]{2,1,0:T(8,128)(2,1)S(1)} %copy-done, s32[32,128]{1,0:T(8,128)S(1)} %bitcast.1, s32[32]{0:T(128)S(1)} %copy-done.5), custom_call_target="tpu_custom_call" | custom-call | tf_op jit(solution)/shard_map/gather_queries/pallas_call | solution.py:421
  14.1 0.0 copy-start.1
  14.1 0.0 copy-start.2
  14.2 0.0 copy-start.3
  14.2 14.7 %attend_pages.1.part_ref = f32[16,9,8,128]{3,2,1,0:T(8,128)S(1)} custom-call(s32[8,384]{1,0:T(8,128)S(1)} %get-tuple-element.7.list_ref, bf16[16,4,16,128]{3,2,1,0:T(8,128)(2,1)S(1)} %get-tuple-element.8.q_ref, bf16[256,4,128,128]{3,2,1,0:T(8,128)(2,1)} %keys.1, bf16[256,4,128,128]{3,2,1,0:T(8,128)(2,1)} %values.1), custom_call_target="tpu_custom_call" | custom-call | tf_op jit(solution)/shard_map/attend_pages/pallas_call | solution.py:440
  28.9 0.0 copy-done.1
  28.9 0.0 copy-done.2
  28.9 0.0 copy-done.3
  28.9 17.2 %exchange_and_finish.1 = bf16[4,16,128]{2,1,0:T(8,128)(2,1)S(1)} custom-call(f32[16,9,8,128]{3,2,1,0:T(8,128)S(1)} %attend_pages.1.part_ref, bf16[4,16,128]{2,1,0:T(8,128)(2,1)S(1)} %copy-done.1, bf16[32,4,128]{2,1,0:T(4,128)(2,1)S(1)} %copy-done.2, bf16[32,4,128]{2,1,0:T(4,128)(2,1)S(1)} %copy-done.3), custom_call_target="tpu_custom_call" | custom-call | tf_op jit(solution)/shard_map/exchange_and_finish/pallas_call | solution.py:462
  46.1 0.6 %copy.9 = bf16[4,16,128]{2,1,0:T(8,128)(2,1)} copy(bf16[4,16,128]{2,1,0:T(8,128)(2,1)S(1)} %exchange_and_finish.1) | data formatting | bytes 32768
Async XLA Ops:
  0.0 0.7 %copy-start = (bf16[4,16,128]{2,1,0:T(8,128)(2,1)S(1)}, bf16[4,16,128]{2,1,0:T(8,128)(2,1)}, u32[]{:S(2)}) copy-start(bf16[4,16,128]{2,1,0:T(8,128)(2,1)} %q_ref.1) | copy-start | bytes 49156
  0.7 0.7 %copy-start.4 = (s32[4096]{0:T(1024)S(1)}, s32[4096]{0:T(1024)}, u32[]{:S(2)}) copy-start(s32[4096]{0:T(1024)} %param.13) | copy-start | bytes 49156
  1.4 0.7 %copy-start.5 = (s32[32]{0:T(128)S(1)}, s32[32]{0:T(128)}, u32[]{:S(2)}) copy-start(s32[32]{0:T(128)} %length_ref.1) | copy-start | bytes 388
  14.1 14.7 %copy-start.1 = (bf16[4,16,128]{2,1,0:T(8,128)(2,1)S(1)}, bf16[4,16,128]{2,1,0:T(8,128)(2,1)}, u32[]{:S(2)}) copy-start(bf16[4,16,128]{2,1,0:T(8,128)(2,1)} %q_ref.1) | copy-start | bytes 49156
  14.1 14.7 %copy-start.2 = (bf16[32,4,128]{2,1,0:T(4,128)(2,1)S(1)}, bf16[32,4,128]{2,1,0:T(4,128)(2,1)}, u32[]{:S(2)}) copy-start(bf16[32,4,128]{2,1,0:T(4,128)(2,1)} %key_ref.1) | copy-start | bytes 98308
  14.2 14.7 %copy-start.3 = (bf16[32,4,128]{2,1,0:T(4,128)(2,1)S(1)}, bf16[32,4,128]{2,1,0:T(4,128)(2,1)}, u32[]{:S(2)}) copy-start(bf16[32,4,128]{2,1,0:T(4,128)(2,1)} %value_ref.1) | copy-start | bytes 98308
where the time goes:
time: 45.9 us; the launch traced here: 46.7 us
  Pallas kernels  43.9 us (96%)
  local copies, waits for them, and re-layouts  2.72 us (6%)
    pallas_call x1, Pallas kernels, on_device(): pl.pallas_call(functools.partial(exchange_kernel, n, plane, parts), out_s...  17.2 us
    pallas_call x1, Pallas kernels, on_device(): pl.pallas_call(functools.partial(attend_kernel, group_rows, blocks), out_...  14.7 us
    pallas_call x1, Pallas kernels, on_device(): pl.pallas_call(functools.partial(gather_kernel, n, pages_here, page_len),...  12 us
    unnamed x13, local copies, waits for them, and re-layouts  2.72 us

commit v1 on v0

v1 whole, which is shorter than its diff:
```python
import functools
import math

import jax
import jax.numpy as jnp
from jax import lax
from jax.experimental import pallas as pl
from jax.experimental.pallas import tpu as pltpu
from jax.sharding import PartitionSpec as P

LOWEST_SCORE = -1e30
MESH = pl.DeviceIdType.MESH
VMEM = pltpu.VMEM

GROUP = 16
RING = 4
LAG = 8
CHUNKS = 4
CODE = 32767.0
TINY = 1e-30

_dot = functools.partial(lax.dot_general, preferred_element_type=jnp.float32)
NT = (((1,), (1,)), ((), ()))
NN = (((1,), (0,)), ((), ()))


def greet(peers):
    barrier = pltpu.get_barrier_semaphore()
    for peer in peers:
        pl.semaphore_signal(barrier, inc=1, device_id={"kv": peer}, device_id_type=MESH)
    return lambda: pl.semaphore_wait(barrier, len(peers))


def split(n):
    plane = min(p for p in range(1, n + 1) if n % p == 0 and p * p >= n)
    return plane, n // plane


def nearest(line, lines):
    if lines & (lines - 1):
        return [lax.rem(line + k, lines) for k in range(1, lines)]
    others = []
    for k in range(1, lines):
        other, bit = line, 1
        while bit < lines:
            if k & bit:
                other = other + bit - 2 * bit * lax.rem(line // bit, 2)
            bit *= 2
        others.append(other)
    return others


def gather_kernel(
    n,
    pages_here,
    page_len,
    fetched,
    spare,
    x_ref,
    table_ref,
    length_ref,
    keys,
    values,
    all_ref,
    list_ref,
    key_ref,
    value_ref,
    table,
    length,
    send_sem,
    recv_sem,
    small_sem,
    page_sem,
):
    me = lax.axis_index("kv")
    plane, lines = split(n)
    spot, line = lax.rem(me, plane), me // plane
    beside = [line * plane + lax.rem(spot + k, plane) for k in range(1, plane)]
    floors = nearest(line, lines)
    arrived = greet(beside + [floor * plane + spot for floor in floors])
    small = [
        pltpu.make_async_copy(x_ref, all_ref.at[me], small_sem.at[0]),
        pltpu.make_async_copy(table_ref, table, small_sem.at[1]),
        pltpu.make_async_copy(length_ref, length, small_sem.at[2]),
    ]
    for copy in small:
        copy.start()
    bulk = []
    for c in range(CHUNKS):
        part = pl.ds(c * (fetched // CHUNKS), fetched // CHUNKS)
        bulk.append(pltpu.make_async_copy(keys.at[part], key_ref.at[part], page_sem.at[0, c]))
        bulk.append(pltpu.make_async_copy(values.at[part], value_ref.at[part], page_sem.at[1, c]))
    for copy in bulk:
        copy.start()
    for copy in small:
        copy.wait()

    def block(source, k, target):
        return pltpu.make_async_remote_copy(
            src_ref=all_ref.at[source],
            dst_ref=all_ref.at[source],
            send_sem=send_sem.at[k],
            recv_sem=recv_sem.at[source],
            device_id={"kv": target},
            device_id_type=MESH,
        )

    state = rank_pages(me, pages_here, page_len, fetched, spare, table, length)
    arrived()
    copies = []

    def send(source, target):
        copy = block(source, len(copies), target)
        copy.start()
        copies.append(copy)

    for floor in floors[::-1]:
        send(me, floor * plane + spot)
    for other in beside:
        send(me, other)
    list_pages(state, list_ref)
    for floor in floors:
        source = floor * plane + spot
        block(source, 0, source).wait_recv()
        for other in beside:
            send(source, other)
    for floor in [line] + floors:
        for k in range(1, plane):
            source = floor * plane + lax.rem(spot + k, plane)
            block(source, 0, source).wait_recv()
    for copy in copies:
        copy.wait_send()
    for copy in bulk:
        copy.wait()


def rank_pages(me, pages_here, page_len, fetched, spare, table_ref, length_ref):
    seqs, slots = table_ref.shape
    page = table_ref[...] - me * pages_here
    line = lax.broadcasted_iota(jnp.int32, (seqs, slots), 0)
    length = jnp.zeros((seqs, slots), jnp.int32)
    for s in range(seqs):
        length = jnp.where(line == s, length_ref[s], length)
    tokens = length - 1 - lax.broadcasted_iota(jnp.int32, (seqs, slots), 1) * page_len
    wanted = (page >= 0) & (page < pages_here) & (tokens > 0)
    ready = wanted & (page < fetched)
    early = jnp.where(ready, 1.0, 0.0)
    late = jnp.where(wanted, 1.0, 0.0) - early
    upto = jnp.where(
        lax.broadcasted_iota(jnp.int32, (slots, slots), 0)
        <= lax.broadcasted_iota(jnp.int32, (slots, slots), 1),
        1.0,
        0.0,
    ).astype(jnp.bfloat16)
    before = jnp.where(
        lax.broadcasted_iota(jnp.int32, (seqs, seqs), 1)
        < lax.broadcasted_iota(jnp.int32, (seqs, seqs), 0),
        1.0,
        0.0,
    ).astype(jnp.bfloat16)

    def place(flag):
        inside = _dot(flag.astype(jnp.bfloat16), upto, NN)
        total = jnp.broadcast_to(jnp.sum(flag, axis=1, keepdims=True), (seqs, slots))
        offset = _dot(before, total.astype(jnp.bfloat16), NN)
        count = jnp.sum(jnp.sum(flag, axis=1, keepdims=True), axis=0, keepdims=True)
        return inside + offset - 1.0, count

    early_rank, early_count = place(early)
    late_rank, late_count = place(late)
    rank = jnp.where(
        ready, early_rank, jnp.where(wanted, late_rank + early_count, -1.0)
    ).astype(jnp.int32)
    ring = fetched + lax.rem(jnp.where(wanted, late_rank, 0.0).astype(jnp.int32), spare)
    wide = jnp.where(wanted, page, 0).astype(jnp.float32)
    slot = jnp.where(ready, page, jnp.where(wanted, ring, 0)).astype(jnp.float32)
    held = jnp.where(wanted, jnp.minimum(tokens, page_len), 0).astype(jnp.float32)
    return rank, wide, slot, held, early_count, early_count + late_count


def list_pages(state, list_ref):
    rank, wide, slot, held, early_count, count = state
    seqs, slots = rank.shape
    listed = list_ref.shape[1]
    row = lax.broadcasted_iota(jnp.int32, (8, slots), 0)
    place = lax.broadcasted_iota(jnp.int32, (listed, slots), 0)
    out = jnp.zeros((8, listed), jnp.float32)
    for s in range(seqs):

        def rows(x):
            return jnp.broadcast_to(x[s : s + 1], (8, slots))

        values = jnp.where(
            row == 0,
            float(s),
            jnp.where(
                row == 1,
                rows(slot),
                jnp.where(row == 2, rows(wide), jnp.where(row == 3, rows(held), 0.0)),
            ),
        ).astype(jnp.bfloat16)
        chosen = jnp.where(
            place == jnp.broadcast_to(rank[s : s + 1], (listed, slots)), 1.0, 0.0
        ).astype(jnp.bfloat16)
        out = out + _dot(values, chosen, NT)
    line = lax.broadcasted_iota(jnp.int32, (8, listed), 0)
    out = jnp.where(line == 4, jnp.broadcast_to(count, (8, listed)), out)
    out = jnp.where(line == 5, jnp.broadcast_to(early_count, (8, listed)), out)
    list_ref[...] = out.astype(jnp.int32)


def attend_kernel(
    group_rows,
    blocks,
    lines,
    list_ref,
    q_ref,
    keys,
    values,
    key_in,
    value_in,
    code_ref,
    stat_ref,
    key_buf,
    value_buf,
    q_wide,
    score,
    best,
    weight,
    total,
    key_sem,
    value_sem,
):
    heads, page_len, width = key_buf.shape[1:]
    seqs = q_wide.shape[0]
    per_block = seqs // blocks
    scale2 = math.log2(math.e) / math.sqrt(width)
    count = list_ref[4, 0]
    early = list_ref[5, 0]
    groups = (count + GROUP - 1) // GROUP
    ready = early // GROUP

    def copies(g, i):
        at = g * GROUP + i
        page, slot, ring = list_ref[2, at], list_ref[1, at], lax.rem(g, RING)
        return (
            pltpu.make_async_copy(keys.at[page], key_buf.at[slot], key_sem.at[ring]),
            pltpu.make_async_copy(values.at[page], value_buf.at[slot], value_sem.at[ring]),
        )

    def whole(g):
        return (g * GROUP >= early) & ((g + 1) * GROUP <= count)

    def mixed(g):
        return jnp.logical_not(whole(g)) & ((g + 1) * GROUP > early)

    def each(g, act):
        def item(i, carry):
            at = g * GROUP + i

            @pl.when((at >= early) & (at < count))
            def _():
                for copy in copies(g, i):
                    act(copy)

            return carry

        lax.fori_loop(0, GROUP, item, 0)

    def start(g):
        @pl.when(whole(g))
        def _():
            for i in range(GROUP):
                for copy in copies(g, i):
                    copy.start()

        @pl.when(mixed(g))
        def _():
            each(g, lambda copy: copy.start())

    def wait(g):
        @pl.when(whole(g))
        def _():
            ring, part = lax.rem(g, RING), pl.ds(0, GROUP)
            pltpu.make_async_copy(keys.at[part], key_buf.at[part], key_sem.at[ring]).wait()
            pltpu.make_async_copy(values.at[part], value_buf.at[part], value_sem.at[ring]).wait()

        @pl.when(mixed(g))
        def _():
            each(g, lambda copy: copy.wait())

    def first(g, carry):
        start(g)
        return carry

    lax.fori_loop(ready, jnp.minimum(groups, ready + RING), first, 0)

    best[...] = jnp.full(best.shape, LOWEST_SCORE, jnp.float32)
    weight[...] = jnp.zeros(weight.shape, jnp.float32)
    total[...] = jnp.zeros(total.shape, jnp.float32)
    rows = q_ref.shape[2]
    for s in range(seqs):
        for pair in range(heads // 2):
            lines_of = []
            for h in (2 * pair, 2 * pair + 1):
                if rows >= group_rows:
                    per = rows // group_rows
                    d, j = s // per, s % per
                    wide = q_ref[d, h].astype(jnp.float32)
                    lines_of.append(wide[j * group_rows : (j + 1) * group_rows])
                else:
                    per = group_rows // rows
                    lines_of += [q_ref[s * per + e, h].astype(jnp.float32) for e in range(per)]
            q_wide[s, pair] = jnp.concatenate(lines_of, axis=0).astype(q_wide.dtype)

    lane = lax.broadcasted_iota(jnp.int32, (group_rows, page_len), 1)
    both = [(i, pair) for i in range(GROUP) for pair in range(heads // 2)]
    every = [(i, h) for i in range(GROUP) for h in range(heads)]

    def ask(g, i, pair):
        seq, slot = list_ref[0, g * GROUP + i], list_ref[1, g * GROUP + i]
        k2 = key_buf[slot, 2 * pair : 2 * pair + 2].reshape(2 * page_len, width)
        found = _dot(q_wide[seq, pair], k2, NT)
        for e in range(2):
            score[i, 2 * pair + e] = found[
                e * group_rows : (e + 1) * group_rows, e * page_len : (e + 1) * page_len
            ]

    def soften(g):
        lengths = [list_ref[3, g * GROUP + i] for i in range(GROUP)]
        scores, tops, weights, keeps, adds = {}, {}, {}, {}, {}
        for i, h in every:
            sc = jnp.where(lane < lengths[i], score[i, h], LOWEST_SCORE)
            scores[i, h] = sc
            tops[i, h] = jnp.broadcast_to(jnp.max(sc, axis=1, keepdims=True), sc.shape)
        for i, h in every:
            seq = list_ref[0, g * GROUP + i]
            found = jnp.where(
                lane < lengths[i], jnp.exp2((scores[i, h] - tops[i, h]) * scale2), 0.0
            )
            old = best[seq, h]
            new = jnp.maximum(old, tops[i, h])
            best[seq, h] = new
            keeps[i, h] = jnp.exp2((old - new) * scale2)
            adds[i, h] = jnp.exp2((tops[i, h] - new) * scale2)
            weight[seq, h] = weight[seq, h] * keeps[i, h] + found * adds[i, h]
            weights[i, h] = found
        return weights, keeps, adds

    def take(g, i, pair, softened):
        weights, keeps, adds = softened
        seq, slot = list_ref[0, g * GROUP + i], list_ref[1, g * GROUP + i]
        w2 = jnp.concatenate([weights[i, 2 * pair], weights[i, 2 * pair + 1]], axis=0)
        v2 = jnp.concatenate([value_buf[slot, 2 * pair], value_buf[slot, 2 * pair + 1]], axis=1)
        found = _dot(w2.astype(jnp.bfloat16), v2, NN)
        for e in range(2):
            h = 2 * pair + e
            mine = found[e * group_rows : (e + 1) * group_rows, e * width : (e + 1) * width]
            total[seq, h] = total[seq, h] * keeps[i, h] + mine * adds[i, h]

    wait(0)
    for i, pair in both:
        ask(0, i, pair)

    def step(g, carry):
        pl.when((g >= ready + 2) & (g + RING - 2 < groups))(lambda: start(g + RING - 2))
        wait(g)
        softened = soften(g - 1)
        for at in range(len(both) + LAG):
            if at >= LAG:
                take(g - 1, *both[at - LAG], softened)
            if at < len(both):
                ask(g, *both[at])
        return carry

    lax.fori_loop(1, groups, step, 0)
    last = jnp.maximum(groups - 1, 0)
    softened = soften(last)
    for i, pair in both:
        take(last, i, pair, softened)

    columns = heads * per_block
    across = blocks // lines
    fit = 128 // (3 * columns)
    stat_lane = lax.broadcasted_iota(jnp.int32, (group_rows, width), 1)
    for a in range(across):
        stats = {}
        for floor in range(lines):
            b = floor * across + a
            tile, base = floor // fit, (floor % fit) * 3 * columns
            stat = stats.get(tile, jnp.zeros((group_rows, width), jnp.float32))
            coded = []
            for c in range(columns):
                h, s = c // per_block, b * per_block + c % per_block
                sums = total[s, h]
                mass = jnp.sum(weight[s, h], axis=1, keepdims=True)
                largest = jnp.maximum(jnp.max(jnp.abs(sums), axis=1, keepdims=True), TINY)
                coded.append(jnp.round(sums * (CODE / largest)))
                stat = jnp.where(stat_lane == base + c, best[s, h], stat)
                stat = jnp.where(
                    stat_lane == base + columns + c, jnp.broadcast_to(mass, stat.shape), stat
                )
                stat = jnp.where(
                    stat_lane == base + 2 * columns + c,
                    jnp.broadcast_to(largest * (1.0 / CODE), stat.shape),
                    stat,
                )
            stats[tile] = stat
            for c in range(0, columns, 2):
                code_ref[b, c * group_rows : (c + 2) * group_rows] = (
                    jnp.concatenate(coded[c : c + 2], axis=0)
                    .astype(jnp.int32)
                    .astype(code_ref.dtype)
                )
        for tile, stat in stats.items():
            stat_ref[a, tile] = stat


def fold(codes, stats, columns, group_rows, scale2):
    top = functools.reduce(jnp.maximum, stats)
    lanes = top.shape[1]
    mass = jnp.zeros_like(top)
    sizes = []
    for stat in stats:
        factor = jnp.exp2((stat - top) * scale2)
        mass = mass + stat * pltpu.roll(factor, columns, 1)
        sizes.append(factor * pltpu.roll(stat, lanes - 2 * columns, 1))
    return top, mass, sizes


def combine(codes, sizes, columns, group_rows):
    sums = [jnp.zeros_like(sizes[0]) for _ in range(columns)]
    for code, size in zip(codes, sizes):
        wide = code[...].astype(jnp.int32).astype(jnp.float32)
        for c in range(columns):
            sums[c] = sums[c] + wide[c * group_rows : (c + 1) * group_rows] * jnp.broadcast_to(
                size[:, c : c + 1], size.shape
            )
    return sums


def exchange_kernel(
    n,
    parts,
    heads,
    code_ref,
    stat_ref,
    q_ref,
    key_ref,
    value_ref,
    out_ref,
    near,
    near_stat,
    folded,
    folded_stat,
    far,
    far_stat,
    near_send,
    near_recv,
    stat_send,
    stat_recv,
    far_send,
    far_recv,
):
    me = lax.axis_index("kv")
    plane, lines = split(n)
    spot, line = lax.rem(me, plane), me // plane
    group_rows, width = stat_ref.shape[2:]
    columns = code_ref.shape[1] // group_rows
    per_block = columns // heads
    across = plane // parts
    fit = 128 // (3 * columns)
    scale2 = math.log2(math.e) / math.sqrt(width)
    spots = [lax.rem(spot + k, plane) for k in range(1, plane)]
    floors = nearest(line, lines)[::-1] + [line]
    arrived = greet([line * plane + p for p in spots] + [f * plane + spot for f in floors[:-1]])

    def stat_copy(p, other, source):
        return pltpu.make_async_remote_copy(
            src_ref=stat_ref.at[other // parts],
            dst_ref=near_stat.at[source],
            send_sem=stat_send.at[p],
            recv_sem=stat_recv.at[source],
            device_id={"kv": line * plane + other},
            device_id_type=MESH,
        )

    def near_copy(k, floor, p, other, source):
        return pltpu.make_async_remote_copy(
            src_ref=code_ref.at[floor * across + other // parts],
            dst_ref=near.at[floor, source],
            send_sem=near_send.at[k, p],
            recv_sem=near_recv.at[floor, source],
            device_id={"kv": line * plane + other},
            device_id_type=MESH,
        )

    def far_copies(k, floor, source):
        return [
            pltpu.make_async_remote_copy(
                src_ref=src.at[k],
                dst_ref=dst.at[source],
                send_sem=far_send.at[e, k],
                recv_sem=far_recv.at[e, source],
                device_id={"kv": floor * plane + spot},
                device_id_type=MESH,
            )
            for e, (src, dst) in enumerate(((folded_stat, far_stat), (folded, far)))
        ]

    arrived()
    copies = []

    def send(copy):
        copy.start()
        copies.append(copy)

    for p, other in enumerate(spots):
        send(stat_copy(p, other, spot))
    for k, floor in enumerate(floors):
        for p, other in enumerate(spots):
            send(near_copy(k, floor, p, other, spot))
    for p, other in enumerate(spots):
        stat_copy(p, other, other).wait_recv()

    def aligned(ref, index, floor):
        if fit >= lines:
            tile, at = ref[index, 0], floor
        else:
            tile, at = ref[index, floor // fit], lax.rem(floor, fit)
        return pltpu.roll(tile, lax.rem(width - at * 3 * columns, width), 1)

    stat_lane = lax.broadcasted_iota(jnp.int32, (group_rows, width), 1)
    own = None
    for k, floor in enumerate(floors):
        stats = [aligned(stat_ref, spot // parts, floor)]
        stats += [aligned(near_stat, other, floor) for other in spots]
        for p, other in enumerate(spots):
            near_copy(k, floor, p, other, other).wait_recv()
        codes = [code_ref.at[floor * across + spot // parts]]
        codes += [near.at[floor, other] for other in spots]
        top, mass, sizes = fold(codes, stats, columns, group_rows, scale2)
        if k == lines - 1:
            own = top, mass, combine(codes, sizes, columns, group_rows)
            break
        size = jnp.maximum(functools.reduce(jnp.add, sizes), TINY)
        inverse = 1.0 / size
        sums = combine(codes, [s * inverse for s in sizes], columns, group_rows)
        folded_stat[k] = jnp.where(
            stat_lane < columns,
            top,
            jnp.where(stat_lane < 2 * columns, mass, pltpu.roll(size, 2 * columns, 1)),
        )
        for c in range(0, columns, 2):
            folded[k, c * group_rows : (c + 2) * group_rows] = (
                jnp.round(jnp.concatenate(sums[c : c + 2], axis=0))
                .astype(jnp.int32)
                .astype(folded.dtype)
            )
        for copy in far_copies(k, floor, line):
            send(copy)
    for k, floor in enumerate(floors[:-1]):
        for copy in far_copies(k, floor, floor):
            copy.wait_recv()
    stats = [far_stat[floor] for floor in floors[:-1]]
    own_top, own_mass, own_sums = own
    top = functools.reduce(jnp.maximum, stats, own_top)
    own_factor = jnp.exp2((own_top - top) * scale2)
    mass = own_mass * pltpu.roll(own_factor, columns, 1)
    sums = [s * jnp.broadcast_to(own_factor[:, c : c + 1], s.shape) for c, s in enumerate(own_sums)]
    sizes = []
    for stat in stats:
        factor = jnp.exp2((stat - top) * scale2)
        mass = mass + stat * pltpu.roll(factor, columns, 1)
        sizes.append(factor * pltpu.roll(stat, width - 2 * columns, 1))
    more = combine([far.at[floor] for floor in floors[:-1]], sizes, columns, group_rows)
    sums = [a + b for a, b in zip(sums, more)]
    for h in range(heads):
        wide = q_ref[h].astype(jnp.float32)
        results = []
        for j in range(per_block):
            c = h * per_block + j
            s = (me // parts) * per_block + j
            rows = slice(j * group_rows, (j + 1) * group_rows) if parts == 1 else slice(None)
            query = wide[rows]
            shape = query.shape
            fresh_key = jnp.broadcast_to(key_ref[s][h : h + 1].astype(jnp.float32), shape)
            fresh_value = jnp.broadcast_to(value_ref[s][h : h + 1].astype(jnp.float32), shape)
            new = jnp.broadcast_to(jnp.sum(query * fresh_key, axis=1, keepdims=True), shape)

            def mine(x):
                if parts == 1:
                    return x
                size = group_rows // parts
                picked = x[:size]
                for p in range(1, parts):
                    picked = jnp.where(
                        lax.rem(me, parts) == p, x[p * size : (p + 1) * size], picked
                    )
                return picked

            old = mine(jnp.broadcast_to(top[:, c : c + 1], top.shape))
            old_mass = mine(jnp.broadcast_to(mass[:, columns + c : columns + c + 1], top.shape))
            old_sum = mine(sums[c])
            highest = jnp.maximum(old, new)
            old_part = jnp.exp2((old - highest) * scale2)
            new_part = jnp.exp2((new - highest) * scale2)
            results.append(
                (old_sum * old_part + new_part * fresh_value) / (old_mass * old_part + new_part)
            )
        out_ref[h] = jnp.concatenate(results, axis=0).astype(out_ref.dtype)
    for copy in copies:
        copy.wait_send()


def far_off(x):
    return pltpu.with_memory_space_constraint(x, pltpu.HBM)


def on_device(n, queries, key_cache, value_cache, key_new, value_new, lengths, page_table):
    heads, local_rows, width = queries.shape
    seqs = lengths.shape[0]
    slots = page_table.shape[0] // seqs
    pages_here, _, page_len, _ = key_cache.shape
    group_rows = local_rows * n // seqs
    parts = max(1, group_rows // local_rows)
    blocks = n // parts
    columns = heads * (seqs // blocks)
    plane, lines = split(n)
    listed = -(-(pages_here + GROUP) // 128) * 128
    fetched = pages_here // 4
    spare = GROUP * RING
    held = fetched + spare
    tiles = -(-lines // (128 // (3 * columns)))
    vmem = pl.BlockSpec(memory_space=VMEM)
    smem = pl.BlockSpec(memory_space=pltpu.SMEM)
    hbm = pl.BlockSpec(memory_space=pltpu.HBM)
    sends = (lines - 1) + (plane - 1) * lines

    every_query, pages, key_buf, value_buf = pl.pallas_call(
        functools.partial(gather_kernel, n, pages_here, page_len, fetched, spare),
        out_shape=(
            jax.ShapeDtypeStruct((n,) + queries.shape, queries.dtype),
            jax.ShapeDtypeStruct((8, listed), jnp.int32),
            VMEM((held,) + key_cache.shape[1:], key_cache.dtype),
            VMEM((held,) + value_cache.shape[1:], value_cache.dtype),
        ),
        in_specs=[hbm] * 5,
        out_specs=(vmem, vmem, vmem, vmem),
        scratch_shapes=[
            VMEM((seqs, slots), jnp.int32),
            pltpu.SMEM((seqs,), jnp.int32),
            pltpu.SemaphoreType.DMA((sends,)),
            pltpu.SemaphoreType.DMA((n,)),
            pltpu.SemaphoreType.DMA((3,)),
            pltpu.SemaphoreType.DMA((2, CHUNKS)),
        ],
        compiler_params=pltpu.CompilerParams(
            collective_id=0, has_side_effects=True, vmem_limit_bytes=6 * 1024 * 1024
        ),
        name="gather_queries",
    )(far_off(queries), far_off(page_table.reshape(seqs, slots)), far_off(lengths), key_cache, value_cache)

    codes, stats, _, _ = pl.pallas_call(
        functools.partial(attend_kernel, group_rows, blocks, lines),
        out_shape=(
            jax.ShapeDtypeStruct((blocks, columns * group_rows, width), jnp.int16),
            jax.ShapeDtypeStruct((plane // parts, tiles, group_rows, width), jnp.float32),
            VMEM(key_buf.shape, key_buf.dtype),
            VMEM(value_buf.shape, value_buf.dtype),
        ),
        in_specs=[smem, vmem, hbm, hbm, vmem, vmem],
        out_specs=(vmem, vmem, vmem, vmem),
        input_output_aliases={4: 2, 5: 3},
        scratch_shapes=[
            VMEM((seqs, heads // 2, 2 * group_rows, width), queries.dtype),
            VMEM((GROUP, heads, group_rows, page_len), jnp.float32),
            VMEM((seqs, heads, group_rows, page_len), jnp.float32),
            VMEM((seqs, heads, group_rows, page_len), jnp.float32),
            VMEM((seqs, heads, group_rows, width), jnp.float32),
            pltpu.SemaphoreType.DMA((RING,)),
            pltpu.SemaphoreType.DMA((RING,)),
        ],
        compiler_params=pltpu.CompilerParams(vmem_limit_bytes=10 * 1024 * 1024),
        name="attend_pages",
    )(pages, every_query, key_cache, value_cache, key_buf, value_buf)

    code = (columns * group_rows, width)
    stat = (group_rows, width)
    return pl.pallas_call(
        functools.partial(exchange_kernel, n, parts, heads),
        out_shape=jax.ShapeDtypeStruct(queries.shape, jnp.bfloat16),
        in_specs=[vmem] * 5,
        out_specs=vmem,
        scratch_shapes=[
            VMEM((lines, plane) + code, jnp.int16),
            VMEM((plane, tiles) + stat, jnp.float32),
            VMEM((lines,) + code, jnp.int16),
            VMEM((lines,) + stat, jnp.float32),
            VMEM((lines,) + code, jnp.int16),
            VMEM((lines,) + stat, jnp.float32),
            pltpu.SemaphoreType.DMA((lines, plane)),
            pltpu.SemaphoreType.DMA((lines, plane)),
            pltpu.SemaphoreType.DMA((plane,)),
            pltpu.SemaphoreType.DMA((plane,)),
            pltpu.SemaphoreType.DMA((2, lines)),
            pltpu.SemaphoreType.DMA((2, lines)),
        ],
        compiler_params=pltpu.CompilerParams(
            collective_id=1, has_side_effects=True, vmem_limit_bytes=16 * 1024 * 1024
        ),
        name="exchange_and_finish",
    )(codes, stats, queries, key_new, value_new)


def solution(mesh):
    placed = (
        P("head", "kv", None),
        P("kv", "head", None, None),
        P("kv", "head", None, None),
        P(None, "head", None),
        P(None, "head", None),
        P(),
        P(),
    )
    return jax.shard_map(
        functools.partial(on_device, mesh.shape["kv"]),
        mesh=mesh,
        in_specs=placed,
        out_specs=P("head", "kv", None),
        check_vma=False,
    )
```

time: 45.9 us -> 39.3 us (0.86); the launches traced: 46.7 us -> 38.9 us
  Pallas kernels: 43.9 us -> 38.2 us
  local copies, waits for them, and re-layouts: 2.72 us -> 0.63 us
    pallas_call x3, Pallas kernels: 43.9 us -> 38.2 us  [the longest x1 16.6 us: on_device(): pl.pallas_call(functools.partial(gather_kernel, n, pages_here, page_len,...]
    unnamed x13 -> x7, local copies, waits for them, and re-layouts: 2.72 us -> 0.63 us
where the time goes in v1:
time: 39.3 us; the launch traced here: 38.9 us
  Pallas kernels  38.2 us (97%)
  local copies, waits for them, and re-layouts  0.63 us (2%)
    pallas_call x1, Pallas kernels, on_device(): pl.pallas_call(functools.partial(gather_kernel, n, pages_here, page_len,...  16.6 us
    pallas_call x1, Pallas kernels, on_device(): pl.pallas_call(functools.partial(attend_kernel, group_rows, blocks, lines...  12.1 us
    pallas_call x1, Pallas kernels, on_device(): pl.pallas_call(functools.partial(exchange_kernel, n, parts, heads), out_s...  9.51 us

profile of v1, /device:TPU:0, one launch (start us, length us, event | category | flops | bytes accessed | tf_op | source)
XLA Modules:
  0.0 38.9 jit_solution(14425613850356631960)
XLA Ops:
  0.0 16.6 %gather_queries.1 = (bf16[16,4,16,128]{3,2,1,0:T(8,128)(2,1)S(1)}, s32[8,384]{1,0:T(8,128)S(1)}, bf16[128,4,128,128]{3,2,1,0:T(8,128)(2,1)S(1)}, bf16[128,4,128,128]{3,2,1,0:T(8,128)(2,1)S(1)}) custom-call(bf16[4,16,128]{2,1,0:T(8,128)(2,1)} %q_ref.1, s32[32,128]{1,0:T(8,128)} %bitcast.1, s32[32]{0:T(128)} %length_ref.1, bf16[256,4,128,128]{3,2,1,0:T(8,128)(2,1)} %keys.3, ...), custom_call_target="tpu_custom_call" | custom-call | tf_op jit(solution)/shard_map/gather_queries/pallas_call | solution.py:640
  16.6 0.0 copy-start
  16.6 0.0 copy-start.1
  16.6 0.0 copy-start.2
  16.7 12.1 %attend_pages.1 = (s16[16,64,128]{2,1,0:T(8,128)(2,1)S(1)}, f32[4,1,8,128]{3,2,1,0:T(8,128)S(1)}, bf16[128,4,128,128]{3,2,1,0:T(8,128)(2,1)S(1)}, bf16[128,4,128,128]{3,2,1,0:T(8,128)(2,1)S(1)}) custom-call(s32[8,384]{1,0:T(8,128)S(1)} %get-tuple-element.11.list_ref, ...), custom_call_target="tpu_custom_call", output_to_operand_aliasing={{2}: (4, {}), {3}: (5, {})} | custom-call | tf_op jit(solution)/shard_map/attend_pages/pallas_call | solution.py:664
  28.8 0.0 copy-done
  28.8 0.0 copy-done.1
  28.8 0.0 copy-done.2
  28.8 9.5 %exchange_and_finish.1 = bf16[4,16,128]{2,1,0:T(8,128)(2,1)S(1)} custom-call(s16[16,64,128]{2,1,0:T(8,128)(2,1)S(1)} %get-tuple-element.15.code_ref, f32[4,1,8,128]{3,2,1,0:T(8,128)S(1)} %get-tuple-element.16.stat_ref, bf16[4,16,128]{2,1,0:T(8,128)(2,1)S(1)} %copy-done, bf16[32,4,128]{2,1,0:T(4,128)(2,1)S(1)} %copy-done.1, bf16[32,4,128]{2,1,0:T(4,128)(2,1)S(1)} %copy-done.2), custom_call_target="tpu_custom_call" | custom-call | tf_op jit(solution)/shard_map/exchange_and_finish/pallas_call | solution.py:690
  38.3 0.6 %copy.13 = bf16[4,16,128]{2,1,0:T(8,128)(2,1)} copy(bf16[4,16,128]{2,1,0:T(8,128)(2,1)S(1)} %exchange_and_finish.1) | data formatting | bytes 32768
Async XLA Ops:
  16.6 12.2 %copy-start = (bf16[4,16,128]{2,1,0:T(8,128)(2,1)S(1)}, bf16[4,16,128]{2,1,0:T(8,128)(2,1)}, u32[]{:S(2)}) copy-start(bf16[4,16,128]{2,1,0:T(8,128)(2,1)} %q_ref.1) | copy-start | bytes 49156
  16.6 12.2 %copy-start.1 = (bf16[32,4,128]{2,1,0:T(4,128)(2,1)S(1)}, bf16[32,4,128]{2,1,0:T(4,128)(2,1)}, u32[]{:S(2)}) copy-start(bf16[32,4,128]{2,1,0:T(4,128)(2,1)} %key_ref.1) | copy-start | bytes 98308
  16.6 12.2 %copy-start.2 = (bf16[32,4,128]{2,1,0:T(4,128)(2,1)S(1)}, bf16[32,4,128]{2,1,0:T(4,128)(2,1)}, u32[]{:S(2)}) copy-start(bf16[32,4,128]{2,1,0:T(4,128)(2,1)} %value_ref.1) | copy-start | bytes 98308

commit v2 on v1

--- a/solution.py
+++ b/solution.py
@@ -12,8 +12,8 @@
 MESH = pl.DeviceIdType.MESH
 VMEM = pltpu.VMEM
 
-GROUP = 16
-RING = 4
+GROUP = 8
+RING = 8
 LAG = 8
 CHUNKS = 4
 CODE = 32767.0
@@ -85,6 +85,8 @@
     ]
     for copy in small:
         copy.start()
+    for copy in small:
+        copy.wait()
     bulk = []
     for c in range(CHUNKS):
         part = pl.ds(c * (fetched // CHUNKS), fetched // CHUNKS)
@@ -92,8 +94,6 @@
         bulk.append(pltpu.make_async_copy(values.at[part], value_ref.at[part], page_sem.at[1, c]))
     for copy in bulk:
         copy.start()
-    for copy in small:
-        copy.wait()
 
     def block(source, k, target):
         return pltpu.make_async_remote_copy(
@@ -105,7 +105,6 @@
             device_id_type=MESH,
         )
 
-    state = rank_pages(me, pages_here, page_len, fetched, spare, table, length)
     arrived()
     copies = []
 
@@ -118,7 +117,7 @@
         send(me, floor * plane + spot)
     for other in beside:
         send(me, other)
-    list_pages(state, list_ref)
+    list_pages(rank_pages(me, pages_here, page_len, fetched, spare, table, length), list_ref)
     for floor in floors:
         source = floor * plane + spot
         block(source, 0, source).wait_recv()
@@ -238,62 +237,50 @@
     count = list_ref[4, 0]
     early = list_ref[5, 0]
     groups = (count + GROUP - 1) // GROUP
-    ready = early // GROUP
-
-    def copies(g, i):
-        at = g * GROUP + i
-        page, slot, ring = list_ref[2, at], list_ref[1, at], lax.rem(g, RING)
+    late = count - early
+    held_groups = (early + GROUP - 1) // GROUP
+    full = late // GROUP
+    rest = lax.rem(late, GROUP)
+
+    def copies(q, i):
+        at = early + q * GROUP + i
+        page, slot, ring = list_ref[2, at], list_ref[1, at], lax.rem(q, RING)
         return (
             pltpu.make_async_copy(keys.at[page], key_buf.at[slot], key_sem.at[ring]),
             pltpu.make_async_copy(values.at[page], value_buf.at[slot], value_sem.at[ring]),
         )
 
-    def whole(g):
-        return (g * GROUP >= early) & ((g + 1) * GROUP <= count)
-
-    def mixed(g):
-        return jnp.logical_not(whole(g)) & ((g + 1) * GROUP > early)
-
-    def each(g, act):
+    def issue(q, i):
+        for copy in copies(q, i):
+            copy.start()
+
+    def some(q, act):
         def item(i, carry):
-            at = g * GROUP + i
-
-            @pl.when((at >= early) & (at < count))
-            def _():
-                for copy in copies(g, i):
-                    act(copy)
-
+            for copy in copies(q, i):
+                act(copy)
             return carry
 
-        lax.fori_loop(0, GROUP, item, 0)
-
-    def start(g):
-        @pl.when(whole(g))
+        lax.fori_loop(0, rest, item, 0)
+
+    def start_rest(q):
+        pl.when((q == full) & (rest > 0))(lambda: some(q, lambda copy: copy.start()))
+
+    def wait(q):
+        @pl.when((q >= 0) & (q < full))
         def _():
-            for i in range(GROUP):
-                for copy in copies(g, i):
-                    copy.start()
-
-        @pl.when(mixed(g))
-        def _():
-            each(g, lambda copy: copy.start())
-
-    def wait(g):
-        @pl.when(whole(g))
-        def _():
-            ring, part = lax.rem(g, RING), pl.ds(0, GROUP)
+            ring, part = lax.rem(q, RING), pl.ds(0, GROUP)
             pltpu.make_async_copy(keys.at[part], key_buf.at[part], key_sem.at[ring]).wait()
             pltpu.make_async_copy(values.at[part], value_buf.at[part], value_sem.at[ring]).wait()
 
-        @pl.when(mixed(g))
-        def _():
-            each(g, lambda copy: copy.wait())
-
-    def first(g, carry):
-        start(g)
+        pl.when((q == full) & (rest > 0))(lambda: some(q, lambda copy: copy.wait()))
+
+    def first(q, carry):
+        for i in range(GROUP):
+            issue(q, i)
         return carry
 
-    lax.fori_loop(ready, jnp.minimum(groups, ready + RING), first, 0)
+    lax.fori_loop(0, jnp.minimum(full, RING), first, 0)
+    pl.when(full < RING)(lambda: start_rest(full))
 
     best[...] = jnp.full(best.shape, LOWEST_SCORE, jnp.float32)
     weight[...] = jnp.zeros(weight.shape, jnp.float32)
@@ -358,22 +345,44 @@
             mine = found[e * group_rows : (e + 1) * group_rows, e * width : (e + 1) * width]
             total[seq, h] = total[seq, h] * keeps[i, h] + mine * adds[i, h]
 
-    wait(0)
+    wait(-(early // GROUP))
     for i, pair in both:
         ask(0, i, pair)
 
-    def step(g, carry):
-        pl.when((g >= ready + 2) & (g + RING - 2 < groups))(lambda: start(g + RING - 2))
-        wait(g)
+    def step(fetch, g, carry):
+        q = g + RING - 2 - held_groups
+        if not fetch:
+            pl.when(q >= RING)(lambda: start_rest(q))
+        wait(g - early // GROUP)
         softened = soften(g - 1)
         for at in range(len(both) + LAG):
             if at >= LAG:
                 take(g - 1, *both[at - LAG], softened)
             if at < len(both):
                 ask(g, *both[at])
+            if fetch and at % 2 and at // 2 < GROUP:
+                issue(q, at // 2)
         return carry
 
-    lax.fori_loop(1, groups, step, 0)
+    steady = jnp.minimum(held_groups + 2, groups)
+    settled = jnp.maximum(full - RING + 2 + held_groups, steady)
+
+    def phase(p, carry):
+        lax.fori_loop(
+            jnp.where(p == 0, 1, settled),
+            jnp.where(p == 0, steady, groups),
+            functools.partial(step, False),
+            0,
+        )
+        lax.fori_loop(
+            jnp.where(p == 0, steady, 0),
+            jnp.where(p == 0, settled, 0),
+            functools.partial(step, True),
+            0,
+        )
+        return carry
+
+    lax.fori_loop(0, 2, phase, 0)
     last = jnp.maximum(groups - 1, 0)
     softened = soften(last)
     for i, pair in both:

time: 39.3 us -> 36.6 us (0.931); the launches traced: 38.9 us -> 37.2 us
  Pallas kernels: 38.2 us -> 36.5 us
    pallas_call x1, Pallas kernels: 16.6 us -> 12.8 us  [on_device(): pl.pallas_call(functools.partial(gather_kernel, n, pages_here, page_len,...]
    pallas_call x1, Pallas kernels: 9.51 us -> 11.8 us  [on_device(): pl.pallas_call(functools.partial(exchange_kernel, n, parts, heads), out_s...]
where the time goes in v2:
time: 36.6 us; the launch traced here: 37.2 us
  Pallas kernels  36.5 us (100%)
  local copies, waits for them, and re-layouts  0.63 us (2%)
    pallas_call x1, Pallas kernels, on_device(): pl.pallas_call(functools.partial(gather_kernel, n, pages_here, page_len,...  12.8 us
    pallas_call x1, Pallas kernels, on_device(): pl.pallas_call(functools.partial(attend_kernel, group_rows, blocks, lines...  11.9 us
    pallas_call x1, Pallas kernels, on_device(): pl.pallas_call(functools.partial(exchange_kernel, n, parts, heads), out_s...  11.8 us

profile of v2, /device:TPU:0, one launch (start us, length us, event | category | flops | bytes accessed | tf_op | source)
XLA Modules:
  0.0 37.2 jit_solution(10996390017950363915)
XLA Ops:
  0.0 12.8 %gather_queries.1 = (bf16[16,4,16,128]{3,2,1,0:T(8,128)(2,1)S(1)}, s32[8,384]{1,0:T(8,128)S(1)}, bf16[128,4,128,128]{3,2,1,0:T(8,128)(2,1)S(1)}, bf16[128,4,128,128]{3,2,1,0:T(8,128)(2,1)S(1)}) custom-call(bf16[4,16,128]{2,1,0:T(8,128)(2,1)} %q_ref.1, s32[32,128]{1,0:T(8,128)} %bitcast.1, s32[32]{0:T(128)} %length_ref.1, bf16[256,4,128,128]{3,2,1,0:T(8,128)(2,1)} %keys.3, ...), custom_call_target="tpu_custom_call" | custom-call | tf_op jit(solution)/shard_map/gather_queries/pallas_call | solution.py:649
  12.8 0.0 copy-start
  12.8 0.0 copy-start.1
  12.8 0.0 copy-start.2
  12.9 11.9 %attend_pages.1 = (s16[16,64,128]{2,1,0:T(8,128)(2,1)S(1)}, f32[4,1,8,128]{3,2,1,0:T(8,128)S(1)}, bf16[128,4,128,128]{3,2,1,0:T(8,128)(2,1)S(1)}, bf16[128,4,128,128]{3,2,1,0:T(8,128)(2,1)S(1)}) custom-call(s32[8,384]{1,0:T(8,128)S(1)} %get-tuple-element.11.list_ref, ...), custom_call_target="tpu_custom_call", output_to_operand_aliasing={{2}: (4, {}), {3}: (5, {})} | custom-call | tf_op jit(solution)/shard_map/attend_pages/pallas_call | solution.py:673
  24.7 0.0 copy-done
  24.7 0.0 copy-done.1
  24.7 0.0 copy-done.2
  24.8 11.8 %exchange_and_finish.1 = bf16[4,16,128]{2,1,0:T(8,128)(2,1)S(1)} custom-call(s16[16,64,128]{2,1,0:T(8,128)(2,1)S(1)} %get-tuple-element.15.code_ref, f32[4,1,8,128]{3,2,1,0:T(8,128)S(1)} %get-tuple-element.16.stat_ref, bf16[4,16,128]{2,1,0:T(8,128)(2,1)S(1)} %copy-done, bf16[32,4,128]{2,1,0:T(4,128)(2,1)S(1)} %copy-done.1, bf16[32,4,128]{2,1,0:T(4,128)(2,1)S(1)} %copy-done.2), custom_call_target="tpu_custom_call" | custom-call | tf_op jit(solution)/shard_map/exchange_and_finish/pallas_call | solution.py:699
  36.6 0.6 %copy.13 = bf16[4,16,128]{2,1,0:T(8,128)(2,1)} copy(bf16[4,16,128]{2,1,0:T(8,128)(2,1)S(1)} %exchange_and_finish.1) | data formatting | bytes 32768
Async XLA Ops:
  12.8 11.9 %copy-start = (bf16[4,16,128]{2,1,0:T(8,128)(2,1)S(1)}, bf16[4,16,128]{2,1,0:T(8,128)(2,1)}, u32[]{:S(2)}) copy-start(bf16[4,16,128]{2,1,0:T(8,128)(2,1)} %q_ref.1) | copy-start | bytes 49156
  12.8 11.9 %copy-start.1 = (bf16[32,4,128]{2,1,0:T(4,128)(2,1)S(1)}, bf16[32,4,128]{2,1,0:T(4,128)(2,1)}, u32[]{:S(2)}) copy-start(bf16[32,4,128]{2,1,0:T(4,128)(2,1)} %key_ref.1) | copy-start | bytes 98308
  12.8 11.9 %copy-start.2 = (bf16[32,4,128]{2,1,0:T(4,128)(2,1)S(1)}, bf16[32,4,128]{2,1,0:T(4,128)(2,1)}, u32[]{:S(2)}) copy-start(bf16[32,4,128]{2,1,0:T(4,128)(2,1)} %value_ref.1) | copy-start | bytes 98308
